TPU v7x, 32 devices: a whole 2x2x4 slice. The times are simulated.
32 devices in a mesh: scan: 2 (over y), ang: 4 (over z), row: 4 (over x, core).
Axes of the slice: x: 2, y: 2, z: 4, core: 2. Of those that a mesh axis runs over, the one named last changes fastest.
Arguments:
- projections: bfloat16 [8, 32, 2560], P(('scan', 'ang'), 'row'), parts along dimension 0, may hold values from 0 to 2
- flats: float32 [64, 2560], P(('scan', 'row')), parts along dimension 0, may hold values from 1 to 3
- block_start: int32 [4, 4], replicated, may hold values from 0 to 2528
- bp_weights: bfloat16 [4, 32, 1024], P(None, None, 'ang'), may hold values from -0.5 to 0.5
Outputs:
- recon: float32 [64, 1024], P(('scan', 'row'), 'ang'), parts along dimension 0
There are 2 independent parts, one for each index of `scan`. A program takes and returns all parts, laid end to end along the dimension named above; an argument that names none is the same for every part. Nothing has to cross between parts.
Inputs may be any that keep to these rules, and one draw needn't show every extreme that they name: block_start[a, r] is the first of the 32 detector columns that pixel region r reads at angle a.
All inputs are finite; a program needn't handle non-finite values.
Results may differ from a plain program's by a relative error of at most 0.009.
Values may be sent and summed in bfloat16 or wider, within the bound.
No kernel may reach another device: no remote copies, remote signals or barrier semaphores. Data moves between devices by JAX's collectives and lax.ppermute only.
A program may use at most 64 MiB of HBM per device.

v0:
```python
import functools

import jax
import jax.numpy as jnp
import numpy as np
from jax import lax
from jax.experimental import pallas as pl
from jax.experimental.pallas import tpu as pltpu
from jax.sharding import PartitionSpec as P


HALO = 4
LANES = 128
RING = (0, 2, 1, 3)
paganin_beta = 8.0
ramp_gain = 320.0


def split(x):
    high = x.astype(jnp.bfloat16)
    low = (x - high.astype(jnp.float32)).astype(jnp.bfloat16)
    return high, low


def sizes(width, rows):
    blocks = width // LANES
    half = blocks // 2 + 1
    return blocks, half, half + -half % 8, rows + 2 * HALO


def wave(j, period):
    y = (2 * j - period).astype(jnp.float32) * np.float32(np.pi / (2 * period))
    z = y * y
    p = np.float32(-1 / 39916800)
    for c in (1 / 362880, -1 / 5040, 1 / 120, -1 / 6, 1.0):
        p = p * z + np.float32(c)
    y = y * p
    return 2.0 * y * y - 1.0


def late(j, period):
    return jnp.where(j >= period // 4, j - period // 4, j + period - period // 4)


def iotas(rows, lanes=LANES):
    return (lax.broadcasted_iota(jnp.int32, (rows, lanes), d) for d in (0, 1))


def matrices(m_high, m_low):
    row, col = iotas(LANES)
    c, s = wave(row * col & (LANES - 1), LANES), wave((row * col - LANES // 4) & (LANES - 1), LANES)
    for ref, c, s in zip((m_high, m_low), split(c), split(s)):
        ref[:LANES, :LANES], ref[:LANES, LANES:] = c, -s
        ref[LANES:, :LANES], ref[LANES:, LANES:] = s, c


def real_dft(x):
    n = len(x)
    h = n // 2
    plus = {a: x[a] + x[n - a] for a in range(1, h)}
    minus = {a: x[a] - x[n - a] for a in range(1, h)}
    re, im = [None] * (h + 1), [None] * (h + 1)

    def total(terms):
        acc = None
        for c, y in terms:
            if abs(c) < 1e-12:
                continue
            z = y if c == 1.0 else (-y if c == -1.0 else y * np.float32(c))
            acc = z if acc is None else acc + z
        return acc

    def cos(m):
        return float(np.round(np.cos(2 * np.pi * (m % n) / n), 15))

    def sin(m):
        return float(np.round(np.sin(2 * np.pi * (m % n) / n), 15))

    for k in range(h // 2 + 1):
        ends = {0: x[0], h: x[h]}
        even = total([(cos(a * k), ends.get(a, plus.get(a))) for a in range(0, h + 1, 2)])
        odd = total([(cos(a * k), ends.get(a, plus.get(a))) for a in range(1, h + 1, 2)])
        re[k] = even if odd is None else even + odd
        re[h - k] = even if odd is None else even - odd
        even = total([(sin(a * k), minus[a]) for a in range(2, h, 2)])
        odd = total([(sin(a * k), minus[a]) for a in range(1, h, 2)])
        parts = [y for y in (even, odd) if y is not None]
        if parts:
            im[k] = -parts[0] if len(parts) == 1 else -(even + odd)
            if h - k != k:
                im[h - k] = (even - odd) if len(parts) == 2 else (even if odd is None else -odd)
    return re, im


def product(passes, high, low, x, m_high, m_low, turned):
    dims = (((1,), (1 if turned else 0,)), ((), ()))
    dot = functools.partial(lax.dot_general, dimension_numbers=dims, preferred_element_type=jnp.float32)
    n = x[0].shape[0]
    for k, part in enumerate(x):
        at = slice(k * n, (k + 1) * n)
        if passes == 1:
            high[at, :] = part.astype(jnp.bfloat16)
        else:
            high[at, :], low[at, :] = split(part)
    out = dot(high[...], m_high)
    if passes > 1:
        out += dot(low[...], m_high)
    if passes > 2:
        out += dot(high[...], m_low)
    return out


def filtered(passes, x, begins, m_high, m_low, kern, turn, high, low, spec):
    rows, blocks = x[0].shape[0], len(x)
    _, half, depth, _ = sizes(blocks * LANES, rows)
    m_high, m_low = m_high[...], m_low[...] if passes > 2 else None
    re, im = real_dft(x)
    parts = []
    for k in range(half):
        c, s = turn[k : k + 1], turn[depth + k : depth + k + 1]
        if im[k] is None:
            parts.append(jnp.concatenate([re[k] * c, -re[k] * s], axis=1))
        else:
            parts.append(jnp.concatenate([re[k] * c + im[k] * s, im[k] * c - re[k] * s], axis=1))
    spec[...] = product(passes, high, low, parts, m_high, m_low, False)
    parts = []
    for k in range(half):
        re = im = None
        for t, begin in enumerate(begins):
            entry = kern[k, pl.ds(begin, rows), :]
            row = k * rows + t
            a, b = entry * spec[row : row + 1, :LANES], entry * spec[row : row + 1, LANES:]
            re, im = (a, b) if re is None else (re + a, im + b)
        parts.append(jnp.concatenate([re, im], axis=1))
    return product(passes, high, low, parts, m_high, m_low, True)


def begin(proj_in, flats_in, starts_in, own, first, second, starts, proj, flats, sems):
    rows, width = own.shape
    pieces = sems.shape[0] // 2
    step = width // pieces
    late = pltpu.make_async_copy(starts_in, starts, sems.at[2 * pieces])
    copies = []
    for i in range(pieces):
        at = pl.ds(i * step, step)
        copies.append(pltpu.make_async_copy(flats_in.at[:, at], flats.at[:, at], sems.at[2 * i]))
        copies.append(pltpu.make_async_copy(proj_in.at[0, :, at], proj.at[:, at], sems.at[2 * i + 1]))
    for copy in (*copies, late):
        copy.start()
    even = lax.rem(lax.axis_index("row"), 2) == 0
    for i in range(pieces):
        copies[2 * i].wait()
        copies[2 * i + 1].wait()
        at = slice(i * step, (i + 1) * step)
        contrast = 1.0 - proj[:, at].astype(jnp.float32) / flats[:, at]
        own[:, at] = contrast
        initial, last = contrast[:HALO], contrast[rows - HALO :]
        first[:, at] = jnp.where(even, last, initial).astype(first.dtype)
        second[:, at] = jnp.where(even, initial, last).astype(second.dtype)
    late.wait()


def each(count, packed, f):
    if packed:
        for i in range(count):
            f(i)
    else:
        pl.loop(0, count)(f)


def prepare(own, m_high, kern, back, turn, jump, high, low, spec, m_low):
    rows, width = own.shape
    blocks, half, depth, tile = sizes(width, rows)
    spread = rows + HALO
    matrices(m_high, m_low)
    k, lane = iotas(depth)
    turn[:depth, :], turn[depth:, :] = wave(k * lane, width), wave(late(k * lane, width), width)
    around = lax.rem(k * lane, blocks)
    jump[:depth, :], jump[depth:, :] = wave(around, blocks), wave(lax.rem(around + blocks - blocks // 4, blocks), blocks)
    v = k + blocks * lane
    folded = jnp.minimum(v, width - v)
    part = jnp.where((k == 0) | (2 * k == blocks), 1.0 / width, 2.0 / width)
    folded_wave = wave(folded, width)
    gain = ramp_gain * (folded.astype(jnp.float32) / width) * (0.5 + 0.5 * folded_wave) * part
    across = 1.0 + paganin_beta * (2.0 - 2.0 * folded_wave)
    u, _ = iotas(tile)
    along = paganin_beta * (2.0 - 2.0 * wave(u, tile))
    parts = [gain[k : k + 1] / (along + across[k : k + 1]) for k in range(half)]
    f_high, f_low = split(jnp.concatenate(parts, axis=1))
    i, u = iotas(2 * spread, tile)
    count = jnp.where(2 * u > tile, 0.0, jnp.where((u == 0) | (2 * u == tile), 1.0 / tile, 2.0 / tile))
    mix_high, mix_low = split(count * wave(lax.rem((i + tile * spread - spread) * u, tile), tile))
    dot = functools.partial(jnp.dot, preferred_element_type=jnp.float32)
    entries = dot(mix_high, f_high) + dot(mix_high, f_low) + dot(mix_low, f_high)
    for k in range(half):
        kern[k] = entries[:, k * LANES : (k + 1) * LANES]
    x = [own[:, LANES * a : LANES * (a + 1)] for a in range(blocks)]
    back[...] = filtered(3, x, [spread - t for t in range(rows)], m_high, m_low, kern, turn, high, low, spec)


def chain(regions, packed, first, second, starts, m_high, kern, own_back, turn, jump, *rest):
    outs, (high, low, spec, back) = rest[:-4], rest[-4:]
    width, rows = first.shape[1], kern.shape[1] // 2 - HALO
    blocks, half, depth, _ = sizes(width, rows)
    spread = rows + HALO
    row, me = lax.axis_index("row"), lax.axis_index("ang")
    even = lax.rem(row, 2) == 0
    got, other = first[...].astype(jnp.float32), second[...].astype(jnp.float32)
    above = jnp.where(row == 0, 0.0, jnp.where(even, other, got))
    below = jnp.where(row == lax.axis_size("row") - 1, 0.0, jnp.where(even, got, other))
    x = jnp.concatenate([above, below], axis=0)
    begins = [spread + HALO - t for t in range(HALO)] + [spread - rows - t for t in range(HALO)]
    x = [x[:, LANES * a : LANES * (a + 1)] for a in range(blocks)]
    back[...] = filtered(PASSES, x, begins, m_high, None, kern, turn, high, low, spec) + own_back[...]
    lanes = lax.broadcasted_iota(jnp.int32, (1, LANES), 1).astype(jnp.float32)
    angle, column = iotas(*starts.shape)
    mine = jnp.where(angle == me, starts[...].astype(jnp.float32), 0.0)
    c, s = turn[:depth, :], turn[depth:, :]

    def region(i):
        start = jnp.where(column == (target(me, i, regions) if packed else i), mine, 0.0)
        start = jnp.sum(jnp.sum(start, axis=1, keepdims=True), axis=0, keepdims=True)
        block = jnp.floor(start * (1.0 / LANES))
        near, far = (jnp.sum(jnp.where(lanes == b, jump[...], 0.0), axis=1, keepdims=True) for b in (block, block + 1.0))
        far = jnp.where(lanes >= start - LANES * block, near, far)
        fc, fs = far[:depth], far[depth:]
        phase = jnp.concatenate([c * fc - s * fs, -(s * fc + c * fs)], axis=0)
        value = None
        for k in range(half):
            v = back[k * rows : (k + 1) * rows, :]
            term = v[:, :LANES] * phase[k : k + 1] + v[:, LANES:] * phase[depth + k : depth + k + 1]
            value = term if value is None else value + term
        if packed:
            outs[i][...] = value.astype(jnp.bfloat16)
        else:
            outs[0][i] = value.astype(jnp.bfloat16)

    each(regions, packed, region)


PASSES = 1
PIECES = 2


def place(angles, packed, starts, weights, placed):
    cb = weights.shape[1]
    me = lax.axis_index("ang")

    def one(i):
        a = source(me, i, angles) if packed else i
        offset = lax.rem(starts[a, me], LANES)
        spot = lax.broadcasted_iota(jnp.int32, (LANES, cb), 0) - lax.broadcasted_iota(jnp.int32, (LANES, cb), 1)
        spot = ((spot == offset) | (spot == offset - LANES)).astype(jnp.float32).astype(jnp.bfloat16)
        value = jnp.dot(spot, weights[a], preferred_element_type=jnp.float32).astype(placed.dtype)
        placed[pl.ds(pl.multiple_of(i * LANES, LANES), LANES) if not packed else pl.ds(i * LANES, LANES), :] = value

    each(angles, packed, one)


def finish(blocks, packed, *refs):
    *cut, placed, out = refs
    dot = functools.partial(jnp.dot, preferred_element_type=jnp.float32)
    if packed:
        out[...] = dot(jnp.concatenate([x[...] for x in cut], axis=1), placed[...])
    else:
        out[...] = jnp.zeros_like(out)

        @pl.loop(0, blocks)
        def _(a):
            out[...] += dot(cut[0][a], placed[pl.ds(pl.multiple_of(a * LANES, LANES), LANES), :])


def rounds(count):
    ring = RING if count == len(RING) else range(count)
    place = {x: p for p, x in enumerate(ring)}
    return [[ring[(place[x] + i) % count] for x in range(count)] for i in range(count)]


def pick(me, values):
    out = jnp.int32(0)
    for x, y in enumerate(values):
        out = jnp.where(me == x, y, out)
    return out


def target(me, i, count):
    return pick(me, rounds(count)[i])


def source(me, i, count):
    return pick(me, rounds(count)[-i % count])


def matchings(count):
    for start in (0, 1):
        ends = [(i, i + 1) for i in range(start, count - 1, 2)]
        if start and count % 2 == 0:
            ends.append((count - 1, 0))
        yield [pair for i, j in ends for pair in ((i, j), (j, i))]


def body(projections, flats, block_start, bp_weights):
    _, rows, width = projections.shape
    angles, _, pixels = bp_weights.shape
    regions, row_count = lax.axis_size("ang"), lax.axis_size("row")
    _, half, depth, _ = sizes(width, rows)
    f32, bf16 = jnp.float32, jnp.bfloat16
    shape = jax.ShapeDtypeStruct
    vmem = pl.BlockSpec(memory_space=pltpu.VMEM)
    limit = pltpu.CompilerParams(vmem_limit_bytes=12 * 1024 * 1024)
    packed = regions <= len(RING)
    pieces = PIECES if width % (PIECES * LANES) == 0 else 1
    hbm = pl.BlockSpec(memory_space=pltpu.HBM)
    contrast, *sent, starts = pl.pallas_call(
        begin,
        out_shape=[shape((rows, width), f32)] + [shape((HALO, width), bf16)] * 2 + [shape(block_start.shape, block_start.dtype)],
        in_specs=[hbm] * 3,
        out_specs=[vmem] * 4,
        scratch_shapes=[
            pltpu.VMEM((rows, width), bf16),
            pltpu.VMEM((rows, width), f32),
            pltpu.SemaphoreType.DMA((2 * pieces + 1,)),
        ],
        compiler_params=limit,
        name="begin",
    )(*(pltpu.with_memory_space_constraint(x, pltpu.HBM) for x in (projections, flats, block_start)))
    scratch = [pltpu.VMEM((half * rows, 2 * LANES), t) for t in (bf16, bf16, f32, f32)]
    work = pl.pallas_call(
        prepare,
        out_shape=[
            shape((2 * LANES, 2 * LANES), bf16),
            shape((half, 2 * (rows + HALO), LANES), f32),
            shape((half * rows, 2 * LANES), f32),
            shape((2 * depth, LANES), f32),
            shape((2 * depth, LANES), f32),
        ],
        in_specs=[vmem],
        out_specs=[vmem] * 5,
        scratch_shapes=scratch[:3] + [pltpu.VMEM((2 * LANES, 2 * LANES), bf16)],
        compiler_params=limit,
        cost_estimate=pl.CostEstimate(flops=400_000_000, bytes_accessed=2_000_000, transcendentals=0),
        name="prepare",
    )
    near, far = matchings(row_count)
    first = lax.ppermute(sent[0], "row", near)

    def edge(contrast, x):
        return x, *work(contrast)

    def inner(contrast, x):
        x = lax.ppermute(x, "row", far)
        return x, *work(contrast)

    row = lax.axis_index("row")
    second, m_high, *ready = lax.cond((row == 0) | (row == row_count - 1), edge, inner, contrast, sent[1])
    cut = pl.pallas_call(
        functools.partial(chain, regions, packed),
        out_shape=[shape((rows, LANES), bf16)] * regions if packed else [shape((regions, rows, LANES), bf16)],
        in_specs=[vmem] * 8,
        out_specs=[vmem] * (regions if packed else 1),
        scratch_shapes=scratch,
        compiler_params=limit,
        name="chain",
    )(first, second, starts, m_high, *ready)
    if packed:
        mine = [cut[0]]
        for i in range(1, regions):
            mine.append(lax.ppermute(cut[i], "ang", list(enumerate(rounds(regions)[i]))))
    else:
        mine = [lax.all_to_all(cut[0], "ang", 0, 0, tiled=True)]
    placed = pl.pallas_call(
        functools.partial(place, angles, packed),
        out_shape=shape((angles * LANES, pixels), bf16),
        in_specs=[pl.BlockSpec(memory_space=pltpu.SMEM), vmem],
        out_specs=vmem,
        compiler_params=limit,
        cost_estimate=pl.CostEstimate(flops=100_000_000, bytes_accessed=400_000, transcendentals=0),
        name="place",
    )(block_start, bp_weights)
    return pl.pallas_call(
        functools.partial(finish, angles, packed),
        out_shape=shape((rows, pixels), f32),
        in_specs=[vmem] * (len(mine) + 1),
        out_specs=vmem,
        compiler_params=limit,
        name="finish",
    )(*mine, placed)


def solution(mesh):
    placed = (P(("scan", "ang"), "row", None), P(("scan", "row"), None), P(), P(None, None, "ang"))
    return jax.shard_map(body, mesh=mesh, in_specs=placed, out_specs=P(("scan", "row"), "ang"), check_vma=False)
```

profile of v0, /device:TPU:2, one launch (start us, length us, event | category | flops | bytes accessed | tf_op | source)
XLA Modules:
  0.0 14.1 jit_solution(13830746183875256525)
XLA Ops:
  0.0 0.9 %begin.1 = (f32[8,2560]{1,0:T(8,128)S(1)}, bf16[4,2560]{1,0:T(4,128)(2,1)S(1)}, bf16[4,2560]{1,0:T(4,128)(2,1)S(1)}, s32[4,4]{1,0:T(4,128)S(1)}) custom-call(bf16[1,8,2560]{2,1,0:T(8,128)(2,1)} %proj_in.1, f32[8,2560]{1,0:T(8,128)} %flats_in.1, s32[4,4]{1,0:T(4,128)} %starts.1), custom_call_target="tpu_custom_call" | custom-call | tf_op jit(solution)/shard_map/begin/pallas_call | solution.py:314
  0.9 0.1 collective-permute-start.1
  1.0 3.3 %conditional.1 = (bf16[4,2560]{1,0:T(4,128)(2,1)S(1)}, bf16[256,256]{1,0:T(8,128)(2,1)S(1)}, f32[11,24,128]{2,1,0:T(8,128)S(1)}, f32[88,256]{1,0:T(8,128)S(1)}, ...) conditional(s32[]{:T(128)} %convert_element_type.3, (bf16[4,2560]{1,0:T(4,128)(2,1)S(1)}, ...), branch_computations={%region_0.0_spmd, %region_1.0_spmd} | conditional | flops 400000000 | bytes 2082008 | solution.py:355
  1.0 0.1 collective-permute-start
  1.1 0.7 %prepare.2 = (bf16[256,256]{1,0:T(8,128)(2,1)S(1)}, f32[11,24,128]{2,1,0:T(8,128)S(1)}, f32[88,256]{1,0:T(8,128)S(1)}, f32[32,128]{1,0:T(8,128)S(1)}, f32[32,128]{1,0:T(8,128)S(1)}) custom-call(f32[8,2560]{1,0:T(8,128)S(1)} %get-tuple-element.14.own), custom_call_target="tpu_custom_call" | custom-call | flops 400000000 | bytes 2000000 | tf_op jit(solution)/shard_map/cond/branch_0_fun/prepare/pallas_call | solution.py:352
  1.8 2.5 %collective-permute-done = bf16[4,2560]{1,0:T(4,128)(2,1)S(1)} collective-permute-done((bf16[4,2560]{1,0:T(4,128)(2,1)S(1)}, bf16[4,2560]{1,0:T(4,128)(2,1)S(1)}, u32[]{:S(2)}, u32[]{:S(2)}) %collective-permute-start) | collective-permute-done | bytes 20512 | tf_op jit(solution)/shard_map/cond/branch_0_fun/ppermute | solution.py:351
  4.3 0.0 collective-permute-done.1.first
  4.3 0.0 copy-start.1
  4.3 0.4 %chain.1 = (bf16[8,128]{1,0:T(8,128)(2,1)S(1)}, bf16[8,128]{1,0:T(8,128)(2,1)S(1)}, bf16[8,128]{1,0:T(8,128)(2,1)S(1)}, bf16[8,128]{1,0:T(8,128)(2,1)S(1)}) custom-call(bf16[4,2560]{1,0:T(4,128)(2,1)S(1)} %collective-permute-done.1.first, bf16[4,2560]{1,0:T(4,128)(2,1)S(1)} %get-tuple-element.44.second, s32[4,4]{1,0:T(4,128)S(1)} %get-tuple-element.45.starts, ...), custom_call_target="tpu_custom_call" | custom-call | tf_op jit(solution)/shard_map/chain/pallas_call | solution.py:356
  4.6 0.0 copy-start
  4.6 2.6 %collective-permute-start.2 = (bf16[8,128]{1,0:T(8,128)(2,1)S(1)}, bf16[8,128]{1,0:T(8,128)(2,1)S(1)}, u32[]{:S(2)}, u32[]{:S(2)}) collective-permute-start(bf16[8,128]{1,0:T(8,128)(2,1)S(1)} %get-tuple-element.52), channel_id=1, source_target_pairs={{0,8},{4,12},{8,4},{12,0},{1,9},{5,13},{9,5},{13,1},{2,10},{6,14},... | collective-permute-start | bytes 6152 | tf_op jit(solution)/shard_map/ppermute | solution.py:368
  7.3 1.6 %collective-permute-start.3 = (bf16[8,128]{1,0:T(8,128)(2,1)S(1)}, bf16[8,128]{1,0:T(8,128)(2,1)S(1)}, u32[]{:S(2)}, u32[]{:S(2)}) collective-permute-start(bf16[8,128]{1,0:T(8,128)(2,1)S(1)} %get-tuple-element.53), channel_id=1, source_target_pairs={{0,4},{4,0},{8,12},{12,8},{1,5},{5,1},{9,13},{13,9},{2,6},{6,2},{1... | collective-permute-start | bytes 6152 | tf_op jit(solution)/shard_map/ppermute | solution.py:368
  8.9 0.3 %collective-permute-start.4 = (bf16[8,128]{1,0:T(8,128)(2,1)S(1)}, bf16[8,128]{1,0:T(8,128)(2,1)S(1)}, u32[]{:S(2)}, u32[]{:S(2)}) collective-permute-start(bf16[8,128]{1,0:T(8,128)(2,1)S(1)} %get-tuple-element.54), channel_id=1, source_target_pairs={{0,12},{4,8},{8,0},{12,4},{1,13},{5,9},{9,1},{13,5},{2,14},{6,10},... | collective-permute-start | bytes 6152 | tf_op jit(solution)/shard_map/ppermute | solution.py:368
  9.2 0.0 copy-done.1
  9.2 0.0 copy-done
  9.2 0.8 %place.1.refs_4_ = bf16[512,256]{1,0:T(8,128)(2,1)S(1)} custom-call(s32[4,4]{1,0:T(4,128)S(1)} %copy-done, bf16[4,32,256]{2,1,0:T(8,128)(2,1)S(1)} %copy-done.1), custom_call_target="tpu_custom_call" | custom-call | flops 100000000 | bytes 400000 | tf_op jit(solution)/shard_map/place/pallas_call | solution.py:371
  10.0 0.1 collective-permute-done.2.refs_1_
  10.1 0.8 %collective-permute-done.3.refs_2_ = bf16[8,128]{1,0:T(8,128)(2,1)S(1)} collective-permute-done((bf16[8,128]{1,0:T(8,128)(2,1)S(1)}, bf16[8,128]{1,0:T(8,128)(2,1)S(1)}, u32[]{:S(2)}, u32[]{:S(2)}) %collective-permute-start.3) | collective-permute-done | bytes 2080 | tf_op jit(solution)/shard_map/ppermute | solution.py:368
  10.9 2.5 %collective-permute-done.4.refs_3_ = bf16[8,128]{1,0:T(8,128)(2,1)S(1)} collective-permute-done((bf16[8,128]{1,0:T(8,128)(2,1)S(1)}, bf16[8,128]{1,0:T(8,128)(2,1)S(1)}, u32[]{:S(2)}, u32[]{:S(2)}) %collective-permute-start.4) | collective-permute-done | bytes 2080 | tf_op jit(solution)/shard_map/ppermute | solution.py:368
  13.3 0.7 %finish.1 = f32[8,256]{1,0:T(8,128)} custom-call(bf16[8,128]{1,0:T(8,128)(2,1)S(1)} %get-tuple-element.51.refs_0_, bf16[8,128]{1,0:T(8,128)(2,1)S(1)} %collective-permute-done.2.refs_1_, bf16[8,128]{1,0:T(8,128)(2,1)S(1)} %collective-permute-done.3.refs_2_, bf16[8,128]{1,0:T(8,128)(2,1)S(1)} %collective-permute-done.4.refs_3_, bf16[512,256]{1,0:T(8,128)(2,1)S(1)} %place.1.refs_4_), custom_call_target="tpu_custom_call" | custom-call | tf_op jit(solution)/shard_map/finish/pallas_call | solution.py:380
Async XLA Ops:
  0.9 3.4 %collective-permute-start.1 = (bf16[4,2560]{1,0:T(4,128)(2,1)S(1)}, bf16[4,2560]{1,0:T(4,128)(2,1)S(1)}, u32[]{:S(2)}, u32[]{:S(2)}) collective-permute-start(bf16[4,2560]{1,0:T(4,128)(2,1)S(1)} %get-tuple-element.41), channel_id=1, source_target_pairs={{0,1},{1,0},{2,3},{3,2},{4,5},{5,4},{6,7},{7,6},{8,9},{9,8},{10,11... | collective-permute-start | bytes 61448 | tf_op jit(solution)/shard_map/ppermute | solution.py:345
  1.0 3.3 %collective-permute-start = (bf16[4,2560]{1,0:T(4,128)(2,1)S(1)}, bf16[4,2560]{1,0:T(4,128)(2,1)S(1)}, u32[]{:S(2)}, u32[]{:S(2)}) collective-permute-start(bf16[4,2560]{1,0:T(4,128)(2,1)S(1)} %get-tuple-element.13), channel_id=1, source_target_pairs={{1,2},{2,1},{3,0},{0,3},{5,6},{6,5},{7,4},{4,7},{9,10},{10,9},{11,... | collective-permute-start | bytes 61448 | tf_op jit(solution)/shard_map/cond/branch_0_fun/ppermute | solution.py:351
  4.3 4.9 %copy-start.1 = (bf16[4,32,256]{2,1,0:T(8,128)(2,1)S(1)}, bf16[4,32,256]{2,1,0:T(8,128)(2,1)}, u32[]{:S(2)}) copy-start(bf16[4,32,256]{2,1,0:T(8,128)(2,1)} %weights.1) | copy-start | bytes 196612
  4.6 4.6 %copy-start = (s32[4,4]{1,0:T(4,128)S(1)}, s32[4,4]{1,0:T(4,128)}, u32[]{:S(2)}) copy-start(s32[4,4]{1,0:T(4,128)} %starts.1) | copy-start | bytes 196
  4.6 5.4 %collective-permute-start.2 = (bf16[8,128]{1,0:T(8,128)(2,1)S(1)}, bf16[8,128]{1,0:T(8,128)(2,1)S(1)}, u32[]{:S(2)}, u32[]{:S(2)}) collective-permute-start(bf16[8,128]{1,0:T(8,128)(2,1)S(1)} %get-tuple-element.52), channel_id=1, source_target_pairs={{0,8},{4,12},{8,4},{12,0},{1,9},{5,13},{9,5},{13,1},{2,10},{6,14},... | collective-permute-start | bytes 6152 | tf_op jit(solution)/shard_map/ppermute | solution.py:368
  7.3 3.6 %collective-permute-start.3 = (bf16[8,128]{1,0:T(8,128)(2,1)S(1)}, bf16[8,128]{1,0:T(8,128)(2,1)S(1)}, u32[]{:S(2)}, u32[]{:S(2)}) collective-permute-start(bf16[8,128]{1,0:T(8,128)(2,1)S(1)} %get-tuple-element.53), channel_id=1, source_target_pairs={{0,4},{4,0},{8,12},{12,8},{1,5},{5,1},{9,13},{13,9},{2,6},{6,2},{1... | collective-permute-start | bytes 6152 | tf_op jit(solution)/shard_map/ppermute | solution.py:368
  8.9 4.5 %collective-permute-start.4 = (bf16[8,128]{1,0:T(8,128)(2,1)S(1)}, bf16[8,128]{1,0:T(8,128)(2,1)S(1)}, u32[]{:S(2)}, u32[]{:S(2)}) collective-permute-start(bf16[8,128]{1,0:T(8,128)(2,1)S(1)} %get-tuple-element.54), channel_id=1, source_target_pairs={{0,12},{4,8},{8,0},{12,4},{1,13},{5,9},{9,1},{13,5},{2,14},{6,10},... | collective-permute-start | bytes 6152 | tf_op jit(solution)/shard_map/ppermute | solution.py:368
where the time goes:
time: 14.3 us; the launch traced here: 14.1 us
  waiting for transfers between devices  5.84 us (41%)
  starting transfers between devices  4.7 us (33%)
  Pallas kernels  3.47 us (24%)
    ppermute x3, starting transfers between devices, body(): lax.ppermute(cut[i], 'ang', list(enumerate(rounds(regions)[i])))  4.55 us
    ppermute x3, waiting for transfers between devices, body(): lax.ppermute(cut[i], 'ang', list(enumerate(rounds(regions)[i])))  3.34 us
    ppermute x1, waiting for transfers between devices, inner(): x = lax.ppermute(x, 'row', far)  2.49 us
    pallas_call x1, Pallas kernels, body(): pl.pallas_call(begin, out_shape=[shape((rows, width), f32)] + [shape((HAL...  0.88 us
    pallas_call x1, Pallas kernels, body(): pl.pallas_call(functools.partial(place, angles, packed), out_shape=shape(...  0.79 us
    pallas_call x1, Pallas kernels, body(): pl.pallas_call(functools.partial(finish, angles, packed), out_shape=shape...  0.75 us
    pallas_call x1, Pallas kernels, inner(): return (x, *work(contrast))  0.69 us
    pallas_call x1, Pallas kernels, body(): pl.pallas_call(functools.partial(chain, regions, packed), out_shape=[shap...  0.36 us
  transfers between devices with their start and end apart: 5, of which 4 were waited for; matrix products, arithmetic and copies ran while one was open for 0% of the time, Pallas kernels for 11%

commit v1 on v0

--- a/solution.py
+++ b/solution.py
@@ -168,7 +168,7 @@
         pl.loop(0, count)(f)
 
 
-def prepare(own, m_high, kern, back, turn, jump, high, low, spec, m_low):
+def prepare(regions, packed, own, starts, m_high, near, back, phases, turn, kern, high, low, spec, m_low):
     rows, width = own.shape
     blocks, half, depth, tile = sizes(width, rows)
     spread = rows + HALO
@@ -176,7 +176,7 @@
     k, lane = iotas(depth)
     turn[:depth, :], turn[depth:, :] = wave(k * lane, width), wave(late(k * lane, width), width)
     around = lax.rem(k * lane, blocks)
-    jump[:depth, :], jump[depth:, :] = wave(around, blocks), wave(lax.rem(around + blocks - blocks // 4, blocks), blocks)
+    jump = jnp.concatenate([wave(around, blocks), wave(lax.rem(around + blocks - blocks // 4, blocks), blocks)], axis=0)
     v = k + blocks * lane
     folded = jnp.minimum(v, width - v)
     part = jnp.where((k == 0) | (2 * k == blocks), 1.0 / width, 2.0 / width)
@@ -192,43 +192,48 @@
     mix_high, mix_low = split(count * wave(lax.rem((i + tile * spread - spread) * u, tile), tile))
     dot = functools.partial(jnp.dot, preferred_element_type=jnp.float32)
     entries = dot(mix_high, f_high) + dot(mix_high, f_low) + dot(mix_low, f_high)
+    row, me = lax.axis_index("row"), lax.axis_index("ang")
+    even = lax.rem(row, 2) == 0
+    inside = (row > 0) & (row < lax.axis_size("row") - 1)
+    reach = rows + HALO - 1
     for k in range(half):
         kern[k] = entries[:, k * LANES : (k + 1) * LANES]
-    x = [own[:, LANES * a : LANES * (a + 1)] for a in range(blocks)]
-    back[...] = filtered(3, x, [spread - t for t in range(rows)], m_high, m_low, kern, turn, high, low, spec)
-
-
-def chain(regions, packed, first, second, starts, m_high, kern, own_back, turn, jump, *rest):
-    outs, (high, low, spec, back) = rest[:-4], rest[-4:]
-    width, rows = first.shape[1], kern.shape[1] // 2 - HALO
-    blocks, half, depth, _ = sizes(width, rows)
-    spread = rows + HALO
-    row, me = lax.axis_index("row"), lax.axis_index("ang")
-    even = lax.rem(row, 2) == 0
-    got, other = first[...].astype(jnp.float32), second[...].astype(jnp.float32)
-    above = jnp.where(row == 0, 0.0, jnp.where(even, other, got))
-    below = jnp.where(row == lax.axis_size("row") - 1, 0.0, jnp.where(even, got, other))
-    x = jnp.concatenate([above, below], axis=0)
-    begins = [spread + HALO - t for t in range(HALO)] + [spread - rows - t for t in range(HALO)]
-    x = [x[:, LANES * a : LANES * (a + 1)] for a in range(blocks)]
-    back[...] = filtered(PASSES, x, begins, m_high, None, kern, turn, high, low, spec) + own_back[...]
+        below, above = kern[k, 1 : 1 + reach, :], kern[k, 2 * spread - reach : 2 * spread, :]
+        near[k, :reach, :] = jnp.where(even, below, above)
+        near[k, 2 * rows : 2 * rows + reach, :] = jnp.where(inside, jnp.where(even, above, below), 0.0)
     lanes = lax.broadcasted_iota(jnp.int32, (1, LANES), 1).astype(jnp.float32)
     angle, column = iotas(*starts.shape)
     mine = jnp.where(angle == me, starts[...].astype(jnp.float32), 0.0)
     c, s = turn[:depth, :], turn[depth:, :]
 
-    def region(i):
+    def phase(i):
         start = jnp.where(column == (target(me, i, regions) if packed else i), mine, 0.0)
         start = jnp.sum(jnp.sum(start, axis=1, keepdims=True), axis=0, keepdims=True)
         block = jnp.floor(start * (1.0 / LANES))
-        near, far = (jnp.sum(jnp.where(lanes == b, jump[...], 0.0), axis=1, keepdims=True) for b in (block, block + 1.0))
-        far = jnp.where(lanes >= start - LANES * block, near, far)
+        here, after = (jnp.sum(jnp.where(lanes == b, jump, 0.0), axis=1, keepdims=True) for b in (block, block + 1.0))
+        far = jnp.where(lanes >= start - LANES * block, here, after)
         fc, fs = far[:depth], far[depth:]
-        phase = jnp.concatenate([c * fc - s * fs, -(s * fc + c * fs)], axis=0)
+        phases[i] = jnp.concatenate([c * fc - s * fs, -(s * fc + c * fs)], axis=0)
+
+    each(regions, packed, phase)
+    x = [own[:, LANES * a : LANES * (a + 1)] for a in range(blocks)]
+    back[...] = filtered(3, x, [spread - t for t in range(rows)], m_high, m_low, kern, turn, high, low, spec)
+
+
+def chain(regions, packed, first, second, m_high, near, own_back, phases, turn, *rest):
+    outs, (high, low, spec, back) = rest[:-4], rest[-4:]
+    width, rows = first.shape[1], near.shape[1] // 4
+    blocks, half, depth, _ = sizes(width, rows)
+    x = jnp.concatenate([first[...].astype(jnp.float32), second[...].astype(jnp.float32)], axis=0)
+    begins = [begin + HALO - 1 - t for begin in (0, 2 * rows) for t in range(HALO)]
+    x = [x[:, LANES * a : LANES * (a + 1)] for a in range(blocks)]
+    back[...] = filtered(PASSES, x, begins, m_high, None, near, turn, high, low, spec) + own_back[...]
+
+    def region(i):
         value = None
         for k in range(half):
             v = back[k * rows : (k + 1) * rows, :]
-            term = v[:, :LANES] * phase[k : k + 1] + v[:, LANES:] * phase[depth + k : depth + k + 1]
+            term = v[:, :LANES] * phases[i, k : k + 1, :] + v[:, LANES:] * phases[i, depth + k : depth + k + 1, :]
             value = term if value is None else value + term
         if packed:
             outs[i][...] = value.astype(jnp.bfloat16)
@@ -326,17 +331,19 @@
     )(*(pltpu.with_memory_space_constraint(x, pltpu.HBM) for x in (projections, flats, block_start)))
     scratch = [pltpu.VMEM((half * rows, 2 * LANES), t) for t in (bf16, bf16, f32, f32)]
     work = pl.pallas_call(
-        prepare,
+        functools.partial(prepare, regions, packed),
         out_shape=[
             shape((2 * LANES, 2 * LANES), bf16),
-            shape((half, 2 * (rows + HALO), LANES), f32),
+            shape((half, 4 * rows, LANES), f32),
             shape((half * rows, 2 * LANES), f32),
-            shape((2 * depth, LANES), f32),
+            shape((regions, 2 * depth, LANES), f32),
             shape((2 * depth, LANES), f32),
         ],
-        in_specs=[vmem],
+        in_specs=[vmem] * 2,
         out_specs=[vmem] * 5,
-        scratch_shapes=scratch[:3] + [pltpu.VMEM((2 * LANES, 2 * LANES), bf16)],
+        scratch_shapes=[pltpu.VMEM((half, 2 * (rows + HALO), LANES), f32)]
+        + scratch[:3]
+        + [pltpu.VMEM((2 * LANES, 2 * LANES), bf16)],
         compiler_params=limit,
         cost_estimate=pl.CostEstimate(flops=400_000_000, bytes_accessed=2_000_000, transcendentals=0),
         name="prepare",
@@ -345,23 +352,23 @@
     first = lax.ppermute(sent[0], "row", near)
 
     def edge(contrast, x):
-        return x, *work(contrast)
+        return x, *work(contrast, starts)
 
     def inner(contrast, x):
         x = lax.ppermute(x, "row", far)
-        return x, *work(contrast)
+        return x, *work(contrast, starts)
 
     row = lax.axis_index("row")
-    second, m_high, *ready = lax.cond((row == 0) | (row == row_count - 1), edge, inner, contrast, sent[1])
+    second, *ready = lax.cond((row == 0) | (row == row_count - 1), edge, inner, contrast, sent[1])
     cut = pl.pallas_call(
         functools.partial(chain, regions, packed),
         out_shape=[shape((rows, LANES), bf16)] * regions if packed else [shape((regions, rows, LANES), bf16)],
-        in_specs=[vmem] * 8,
+        in_specs=[vmem] * 7,
         out_specs=[vmem] * (regions if packed else 1),
         scratch_shapes=scratch,
         compiler_params=limit,
         name="chain",
-    )(first, second, starts, m_high, *ready)
+    )(first, second, *ready)
     if packed:
         mine = [cut[0]]
         for i in range(1, regions):

time: 14.3 us -> 14.3 us (level)
  transfers between devices with their start and end apart: 5 -> 5, of which waited for: 4 -> 4; matrix products, arithmetic and copies ran while one was open for 0% -> 0% of each run, Pallas kernels for 11% -> 10%
where the time goes in v1:
time: 14.3 us; the launch traced here: 14.1 us
  waiting for transfers between devices  5.86 us (41%)
  starting transfers between devices  4.7 us (33%)
  Pallas kernels  3.44 us (24%)
    ppermute x3, starting transfers between devices, body(): lax.ppermute(cut[i], 'ang', list(enumerate(rounds(regions)[i])))  4.55 us
    ppermute x3, waiting for transfers between devices, body(): lax.ppermute(cut[i], 'ang', list(enumerate(rounds(regions)[i])))  3.35 us
    ppermute x1, waiting for transfers between devices, inner(): x = lax.ppermute(x, 'row', far)  2.51 us
    pallas_call x1, Pallas kernels, body(): pl.pallas_call(begin, out_shape=[shape((rows, width), f32)] + [shape((HAL...  0.88 us
    pallas_call x1, Pallas kernels, body(): pl.pallas_call(functools.partial(place, angles, packed), out_shape=shape(...  0.79 us
    pallas_call x1, Pallas kernels, body(): pl.pallas_call(functools.partial(finish, angles, packed), out_shape=shape...  0.75 us
    pallas_call x1, Pallas kernels, inner(): return (x, *work(contrast, starts))  0.68 us
    pallas_call x1, Pallas kernels, body(): pl.pallas_call(functools.partial(chain, regions, packed), out_shape=[shap...  0.34 us
  transfers between devices with their start and end apart: 5, of which 4 were waited for; matrix products, arithmetic and copies ran while one was open for 0% of the time, Pallas kernels for 10%

profile of v1, /device:TPU:2, one launch (start us, length us, event | category | flops | bytes accessed | tf_op | source)
XLA Modules:
  0.0 14.1 jit_solution(16097590467289443136)
XLA Ops:
  0.0 0.9 %begin.1 = (f32[8,2560]{1,0:T(8,128)S(1)}, bf16[4,2560]{1,0:T(4,128)(2,1)S(1)}, bf16[4,2560]{1,0:T(4,128)(2,1)S(1)}, s32[4,4]{1,0:T(4,128)S(1)}) custom-call(bf16[1,8,2560]{2,1,0:T(8,128)(2,1)} %proj_in.1, f32[8,2560]{1,0:T(8,128)} %flats_in.1, s32[4,4]{1,0:T(4,128)} %starts.1), custom_call_target="tpu_custom_call" | custom-call | tf_op jit(solution)/shard_map/begin/pallas_call | solution.py:319
  0.9 0.1 collective-permute-start.1
  1.0 3.3 %conditional.1 = (bf16[4,2560]{1,0:T(4,128)(2,1)S(1)}, bf16[256,256]{1,0:T(8,128)(2,1)S(1)}, f32[11,32,128]{2,1,0:T(8,128)S(1)}, f32[88,256]{1,0:T(8,128)S(1)}, ...) conditional(s32[]{:T(128)} %convert_element_type.3, (bf16[4,2560]{1,0:T(4,128)(2,1)S(1)}, ...), branch_computations={%region_0.0_spmd, %region_1.0_spmd} | conditional | flops 400000000 | bytes 2082008 | solution.py:362
  1.0 0.1 collective-permute-start
  1.1 0.7 %prepare.2 = (bf16[256,256]{1,0:T(8,128)(2,1)S(1)}, f32[11,32,128]{2,1,0:T(8,128)S(1)}, f32[88,256]{1,0:T(8,128)S(1)}, f32[4,32,128]{2,1,0:T(8,128)S(1)}, f32[32,128]{1,0:T(8,128)S(1)}) custom-call(f32[8,2560]{1,0:T(8,128)S(1)} %get-tuple-element.18.own, s32[4,4]{1,0:T(4,128)S(1)} %get-tuple-element.19.starts), custom_call_target="tpu_custom_call" | custom-call | flops 400000000 | bytes 2000000 | tf_op jit(solution)/shard_map/cond/branch_0_fun/prepare/pallas_call | solution.py:359
  1.7 2.5 %collective-permute-done = bf16[4,2560]{1,0:T(4,128)(2,1)S(1)} collective-permute-done((bf16[4,2560]{1,0:T(4,128)(2,1)S(1)}, bf16[4,2560]{1,0:T(4,128)(2,1)S(1)}, u32[]{:S(2)}, u32[]{:S(2)}) %collective-permute-start) | collective-permute-done | bytes 20512 | tf_op jit(solution)/shard_map/cond/branch_0_fun/ppermute | solution.py:358
  4.3 0.0 collective-permute-done.1.first
  4.3 0.0 copy-start.1
  4.3 0.3 %chain.1 = (bf16[8,128]{1,0:T(8,128)(2,1)S(1)}, bf16[8,128]{1,0:T(8,128)(2,1)S(1)}, bf16[8,128]{1,0:T(8,128)(2,1)S(1)}, bf16[8,128]{1,0:T(8,128)(2,1)S(1)}) custom-call(bf16[4,2560]{1,0:T(4,128)(2,1)S(1)} %collective-permute-done.1.first, bf16[4,2560]{1,0:T(4,128)(2,1)S(1)} %get-tuple-element.51.second, bf16[256,256]{1,0:T(8,128)(2,1)S(1)} %get-tuple-element.52.m_high, ...), custom_call_target="tpu_custom_call" | custom-call | tf_op jit(solution)/shard_map/chain/pallas_call | solution.py:363
  4.6 0.0 copy-start
  4.6 2.6 %collective-permute-start.2 = (bf16[8,128]{1,0:T(8,128)(2,1)S(1)}, bf16[8,128]{1,0:T(8,128)(2,1)S(1)}, u32[]{:S(2)}, u32[]{:S(2)}) collective-permute-start(bf16[8,128]{1,0:T(8,128)(2,1)S(1)} %get-tuple-element.58), channel_id=1, source_target_pairs={{0,8},{4,12},{8,4},{12,0},{1,9},{5,13},{9,5},{13,1},{2,10},{6,14},... | collective-permute-start | bytes 6152 | tf_op jit(solution)/shard_map/ppermute | solution.py:375
  7.3 1.6 %collective-permute-start.3 = (bf16[8,128]{1,0:T(8,128)(2,1)S(1)}, bf16[8,128]{1,0:T(8,128)(2,1)S(1)}, u32[]{:S(2)}, u32[]{:S(2)}) collective-permute-start(bf16[8,128]{1,0:T(8,128)(2,1)S(1)} %get-tuple-element.59), channel_id=1, source_target_pairs={{0,4},{4,0},{8,12},{12,8},{1,5},{5,1},{9,13},{13,9},{2,6},{6,2},{1... | collective-permute-start | bytes 6152 | tf_op jit(solution)/shard_map/ppermute | solution.py:375
  8.8 0.3 %collective-permute-start.4 = (bf16[8,128]{1,0:T(8,128)(2,1)S(1)}, bf16[8,128]{1,0:T(8,128)(2,1)S(1)}, u32[]{:S(2)}, u32[]{:S(2)}) collective-permute-start(bf16[8,128]{1,0:T(8,128)(2,1)S(1)} %get-tuple-element.60), channel_id=1, source_target_pairs={{0,12},{4,8},{8,0},{12,4},{1,13},{5,9},{9,1},{13,5},{2,14},{6,10},... | collective-permute-start | bytes 6152 | tf_op jit(solution)/shard_map/ppermute | solution.py:375
  9.2 0.0 copy-done.1
  9.2 0.0 copy-done
  9.2 0.8 %place.1.refs_4_ = bf16[512,256]{1,0:T(8,128)(2,1)S(1)} custom-call(s32[4,4]{1,0:T(4,128)S(1)} %copy-done, bf16[4,32,256]{2,1,0:T(8,128)(2,1)S(1)} %copy-done.1), custom_call_target="tpu_custom_call" | custom-call | flops 100000000 | bytes 400000 | tf_op jit(solution)/shard_map/place/pallas_call | solution.py:378
  10.0 0.1 collective-permute-done.2.refs_1_
  10.1 0.8 %collective-permute-done.3.refs_2_ = bf16[8,128]{1,0:T(8,128)(2,1)S(1)} collective-permute-done((bf16[8,128]{1,0:T(8,128)(2,1)S(1)}, bf16[8,128]{1,0:T(8,128)(2,1)S(1)}, u32[]{:S(2)}, u32[]{:S(2)}) %collective-permute-start.3) | collective-permute-done | bytes 2080 | tf_op jit(solution)/shard_map/ppermute | solution.py:375
  10.9 2.5 %collective-permute-done.4.refs_3_ = bf16[8,128]{1,0:T(8,128)(2,1)S(1)} collective-permute-done((bf16[8,128]{1,0:T(8,128)(2,1)S(1)}, bf16[8,128]{1,0:T(8,128)(2,1)S(1)}, u32[]{:S(2)}, u32[]{:S(2)}) %collective-permute-start.4) | collective-permute-done | bytes 2080 | tf_op jit(solution)/shard_map/ppermute | solution.py:375
  13.3 0.7 %finish.1 = f32[8,256]{1,0:T(8,128)} custom-call(bf16[8,128]{1,0:T(8,128)(2,1)S(1)} %get-tuple-element.57.refs_0_, bf16[8,128]{1,0:T(8,128)(2,1)S(1)} %collective-permute-done.2.refs_1_, bf16[8,128]{1,0:T(8,128)(2,1)S(1)} %collective-permute-done.3.refs_2_, bf16[8,128]{1,0:T(8,128)(2,1)S(1)} %collective-permute-done.4.refs_3_, bf16[512,256]{1,0:T(8,128)(2,1)S(1)} %place.1.refs_4_), custom_call_target="tpu_custom_call" | custom-call | tf_op jit(solution)/shard_map/finish/pallas_call | solution.py:387
Async XLA Ops:
  0.9 3.4 %collective-permute-start.1 = (bf16[4,2560]{1,0:T(4,128)(2,1)S(1)}, bf16[4,2560]{1,0:T(4,128)(2,1)S(1)}, u32[]{:S(2)}, u32[]{:S(2)}) collective-permute-start(bf16[4,2560]{1,0:T(4,128)(2,1)S(1)} %get-tuple-element.47), channel_id=1, source_target_pairs={{0,1},{1,0},{2,3},{3,2},{4,5},{5,4},{6,7},{7,6},{8,9},{9,8},{10,11... | collective-permute-start | bytes 61448 | tf_op jit(solution)/shard_map/ppermute | solution.py:352
  1.0 3.3 %collective-permute-start = (bf16[4,2560]{1,0:T(4,128)(2,1)S(1)}, bf16[4,2560]{1,0:T(4,128)(2,1)S(1)}, u32[]{:S(2)}, u32[]{:S(2)}) collective-permute-start(bf16[4,2560]{1,0:T(4,128)(2,1)S(1)} %get-tuple-element.17), channel_id=1, source_target_pairs={{1,2},{2,1},{3,0},{0,3},{5,6},{6,5},{7,4},{4,7},{9,10},{10,9},{11,... | collective-permute-start | bytes 61448 | tf_op jit(solution)/shard_map/cond/branch_0_fun/ppermute | solution.py:358
  4.3 4.9 %copy-start.1 = (bf16[4,32,256]{2,1,0:T(8,128)(2,1)S(1)}, bf16[4,32,256]{2,1,0:T(8,128)(2,1)}, u32[]{:S(2)}) copy-start(bf16[4,32,256]{2,1,0:T(8,128)(2,1)} %weights.1) | copy-start | bytes 196612
  4.6 4.6 %copy-start = (s32[4,4]{1,0:T(4,128)S(1)}, s32[4,4]{1,0:T(4,128)}, u32[]{:S(2)}) copy-start(s32[4,4]{1,0:T(4,128)} %starts.1) | copy-start | bytes 196
  4.6 5.4 %collective-permute-start.2 = (bf16[8,128]{1,0:T(8,128)(2,1)S(1)}, bf16[8,128]{1,0:T(8,128)(2,1)S(1)}, u32[]{:S(2)}, u32[]{:S(2)}) collective-permute-start(bf16[8,128]{1,0:T(8,128)(2,1)S(1)} %get-tuple-element.58), channel_id=1, source_target_pairs={{0,8},{4,12},{8,4},{12,0},{1,9},{5,13},{9,5},{13,1},{2,10},{6,14},... | collective-permute-start | bytes 6152 | tf_op jit(solution)/shard_map/ppermute | solution.py:375
  7.3 3.6 %collective-permute-start.3 = (bf16[8,128]{1,0:T(8,128)(2,1)S(1)}, bf16[8,128]{1,0:T(8,128)(2,1)S(1)}, u32[]{:S(2)}, u32[]{:S(2)}) collective-permute-start(bf16[8,128]{1,0:T(8,128)(2,1)S(1)} %get-tuple-element.59), channel_id=1, source_target_pairs={{0,4},{4,0},{8,12},{12,8},{1,5},{5,1},{9,13},{13,9},{2,6},{6,2},{1... | collective-permute-start | bytes 6152 | tf_op jit(solution)/shard_map/ppermute | solution.py:375
  8.8 4.5 %collective-permute-start.4 = (bf16[8,128]{1,0:T(8,128)(2,1)S(1)}, bf16[8,128]{1,0:T(8,128)(2,1)S(1)}, u32[]{:S(2)}, u32[]{:S(2)}) collective-permute-start(bf16[8,128]{1,0:T(8,128)(2,1)S(1)} %get-tuple-element.60), channel_id=1, source_target_pairs={{0,12},{4,8},{8,0},{12,4},{1,13},{5,9},{9,1},{13,5},{2,14},{6,10},... | collective-permute-start | bytes 6152 | tf_op jit(solution)/shard_map/ppermute | solution.py:375

commit v2 on v1

--- a/solution.py
+++ b/solution.py
@@ -12,6 +12,8 @@
 HALO = 4
 LANES = 128
 RING = (0, 2, 1, 3)
+LAST = 2
+FIRST = (0, 1, 3)
 paganin_beta = 8.0
 ramp_gain = 320.0
 
@@ -122,14 +124,15 @@
             parts.append(jnp.concatenate([re[k] * c, -re[k] * s], axis=1))
         else:
             parts.append(jnp.concatenate([re[k] * c + im[k] * s, im[k] * c - re[k] * s], axis=1))
-    spec[...] = product(passes, high, low, parts, m_high, m_low, False)
+    whole = product(passes, high, low, parts, m_high, m_low, False)
+    spec[...] = whole
     parts = []
     for k in range(half):
         re = im = None
         for t, begin in enumerate(begins):
             entry = kern[k, pl.ds(begin, rows), :]
             row = k * rows + t
-            a, b = entry * spec[row : row + 1, :LANES], entry * spec[row : row + 1, LANES:]
+            a, b = entry * whole[row : row + 1, :LANES], entry * spec[row : row + 1, LANES:]
             re, im = (a, b) if re is None else (re + a, im + b)
         parts.append(jnp.concatenate([re, im], axis=1))
     return product(passes, high, low, parts, m_high, m_low, True)
@@ -145,8 +148,8 @@
         at = pl.ds(i * step, step)
         copies.append(pltpu.make_async_copy(flats_in.at[:, at], flats.at[:, at], sems.at[2 * i]))
         copies.append(pltpu.make_async_copy(proj_in.at[0, :, at], proj.at[:, at], sems.at[2 * i + 1]))
-    for copy in (*copies, late):
-        copy.start()
+    for k, copy in enumerate((*copies, late)):
+        copy.start(priority=k % 2)
     even = lax.rem(lax.axis_index("row"), 2) == 0
     for i in range(pieces):
         copies[2 * i].wait()
@@ -262,11 +265,21 @@
     each(angles, packed, one)
 
 
+def partial(*refs):
+    *cut, placed, out = refs
+    total = None
+    for i, x in zip(FIRST, cut):
+        term = jnp.dot(x[...], placed[i * LANES : (i + 1) * LANES, :], preferred_element_type=jnp.float32)
+        total = term if total is None else total + term
+    out[...] = total
+
+
 def finish(blocks, packed, *refs):
     *cut, placed, out = refs
     dot = functools.partial(jnp.dot, preferred_element_type=jnp.float32)
     if packed:
-        out[...] = dot(jnp.concatenate([x[...] for x in cut], axis=1), placed[...])
+        last, part = cut
+        out[...] = part[...] + dot(last[...], placed[LAST * LANES : (LAST + 1) * LANES, :])
     else:
         out[...] = jnp.zeros_like(out)
 
@@ -313,7 +326,8 @@
     shape = jax.ShapeDtypeStruct
     vmem = pl.BlockSpec(memory_space=pltpu.VMEM)
     limit = pltpu.CompilerParams(vmem_limit_bytes=12 * 1024 * 1024)
-    packed = regions <= len(RING)
+    packing = pltpu.CompilerParams(vmem_limit_bytes=12 * 1024 * 1024)
+    packed = regions == len(RING)
     pieces = PIECES if width % (PIECES * LANES) == 0 else 1
     hbm = pl.BlockSpec(memory_space=pltpu.HBM)
     contrast, *sent, starts = pl.pallas_call(
@@ -344,7 +358,7 @@
         scratch_shapes=[pltpu.VMEM((half, 2 * (rows + HALO), LANES), f32)]
         + scratch[:3]
         + [pltpu.VMEM((2 * LANES, 2 * LANES), bf16)],
-        compiler_params=limit,
+        compiler_params=packing,
         cost_estimate=pl.CostEstimate(flops=400_000_000, bytes_accessed=2_000_000, transcendentals=0),
         name="prepare",
     )
@@ -366,7 +380,7 @@
         in_specs=[vmem] * 7,
         out_specs=[vmem] * (regions if packed else 1),
         scratch_shapes=scratch,
-        compiler_params=limit,
+        compiler_params=packing,
         name="chain",
     )(first, second, *ready)
     if packed:
@@ -384,6 +398,16 @@
         cost_estimate=pl.CostEstimate(flops=100_000_000, bytes_accessed=400_000, transcendentals=0),
         name="place",
     )(block_start, bp_weights)
+    if packed:
+        part = pl.pallas_call(
+            partial,
+            out_shape=shape((rows, pixels), f32),
+            in_specs=[vmem] * (len(FIRST) + 1),
+            out_specs=vmem,
+            compiler_params=limit,
+            name="partial",
+        )(*(mine[i] for i in FIRST), placed)
+        mine = [mine[LAST], part]
     return pl.pallas_call(
         functools.partial(finish, angles, packed),
         out_shape=shape((rows, pixels), f32),

time: 14.3 us -> 14.4 us (level)
  starting transfers between devices: 4.7 us -> 5.61 us
  waiting for transfers between devices: 5.86 us -> 4.97 us
    ppermute x3, starting transfers between devices: 4.55 us -> 5.47 us  [body(): lax.ppermute(cut[i], 'ang', list(enumerate(rounds(regions)[i])))]
    ppermute x3, waiting for transfers between devices: 3.35 us -> 2.45 us  [body(): lax.ppermute(cut[i], 'ang', list(enumerate(rounds(regions)[i])))]
  transfers between devices with their start and end apart: 5 -> 5, of which waited for: 4 -> 3; matrix products, arithmetic and copies ran while one was open for 0% -> 0% of each run, Pallas kernels for 10% -> 11%
where the time goes in v2:
time: 14.4 us; the launch traced here: 14.2 us
  starting transfers between devices  5.61 us (39%)
  waiting for transfers between devices  4.97 us (35%)
  Pallas kernels  3.56 us (25%)
    ppermute x3, starting transfers between devices, body(): lax.ppermute(cut[i], 'ang', list(enumerate(rounds(regions)[i])))  5.47 us
    ppermute x1, waiting for transfers between devices, inner(): x = lax.ppermute(x, 'row', far)  2.52 us
    ppermute x3, waiting for transfers between devices, body(): lax.ppermute(cut[i], 'ang', list(enumerate(rounds(regions)[i])))  2.45 us
    pallas_call x1, Pallas kernels, body(): pl.pallas_call(begin, out_shape=[shape((rows, width), f32)] + [shape((HAL...  0.88 us
    pallas_call x1, Pallas kernels, body(): pl.pallas_call(functools.partial(place, angles, packed), out_shape=shape(...  0.79 us
    pallas_call x1, Pallas kernels, body(): pl.pallas_call(functools.partial(finish, angles, packed), out_shape=shape...  0.76 us
    pallas_call x1, Pallas kernels, inner(): return (x, *work(contrast, starts))  0.67 us
    pallas_call x1, Pallas kernels, body(): pl.pallas_call(functools.partial(chain, regions, packed), out_shape=[shap...  0.34 us
  transfers between devices with their start and end apart: 5, of which 3 were waited for; matrix products, arithmetic and copies ran while one was open for 0% of the time, Pallas kernels for 11%

profile of v2, /device:TPU:2, one launch (start us, length us, event | category | flops | bytes accessed | tf_op | source)
XLA Modules:
  0.0 14.2 jit_solution(13796017621700581562)
XLA Ops:
  0.0 0.9 %begin.1 = (f32[8,2560]{1,0:T(8,128)S(1)}, bf16[4,2560]{1,0:T(4,128)(2,1)S(1)}, bf16[4,2560]{1,0:T(4,128)(2,1)S(1)}, s32[4,4]{1,0:T(4,128)S(1)}) custom-call(bf16[1,8,2560]{2,1,0:T(8,128)(2,1)} %proj_in.1, f32[8,2560]{1,0:T(8,128)} %flats_in.1, s32[4,4]{1,0:T(4,128)} %starts.1), custom_call_target="tpu_custom_call" | custom-call | tf_op jit(solution)/shard_map/begin/pallas_call | solution.py:333
  0.9 0.1 collective-permute-start.1
  1.0 3.3 %conditional.1 = (bf16[4,2560]{1,0:T(4,128)(2,1)S(1)}, bf16[256,256]{1,0:T(8,128)(2,1)S(1)}, f32[11,32,128]{2,1,0:T(8,128)S(1)}, f32[88,256]{1,0:T(8,128)S(1)}, ...) conditional(s32[]{:T(128)} %convert_element_type.3, (bf16[4,2560]{1,0:T(4,128)(2,1)S(1)}, ...), branch_computations={%region_0.0_spmd, %region_1.0_spmd} | conditional | flops 400000000 | bytes 2082008 | solution.py:376
  1.0 0.1 collective-permute-start
  1.1 0.7 %prepare.2 = (bf16[256,256]{1,0:T(8,128)(2,1)S(1)}, f32[11,32,128]{2,1,0:T(8,128)S(1)}, f32[88,256]{1,0:T(8,128)S(1)}, f32[4,32,128]{2,1,0:T(8,128)S(1)}, f32[32,128]{1,0:T(8,128)S(1)}) custom-call(f32[8,2560]{1,0:T(8,128)S(1)} %get-tuple-element.18.own, s32[4,4]{1,0:T(4,128)S(1)} %get-tuple-element.19.starts), custom_call_target="tpu_custom_call" | custom-call | flops 400000000 | bytes 2000000 | tf_op jit(solution)/shard_map/cond/branch_0_fun/prepare/pallas_call | solution.py:373
  1.7 2.5 %collective-permute-done = bf16[4,2560]{1,0:T(4,128)(2,1)S(1)} collective-permute-done((bf16[4,2560]{1,0:T(4,128)(2,1)S(1)}, bf16[4,2560]{1,0:T(4,128)(2,1)S(1)}, u32[]{:S(2)}, u32[]{:S(2)}) %collective-permute-start) | collective-permute-done | bytes 20512 | tf_op jit(solution)/shard_map/cond/branch_0_fun/ppermute | solution.py:372
  4.3 0.0 collective-permute-done.1.first
  4.3 0.0 copy-start.1
  4.3 0.3 %chain.1 = (bf16[8,128]{1,0:T(8,128)(2,1)S(1)}, bf16[8,128]{1,0:T(8,128)(2,1)S(1)}, bf16[8,128]{1,0:T(8,128)(2,1)S(1)}, bf16[8,128]{1,0:T(8,128)(2,1)S(1)}) custom-call(bf16[4,2560]{1,0:T(4,128)(2,1)S(1)} %collective-permute-done.1.first, bf16[4,2560]{1,0:T(4,128)(2,1)S(1)} %get-tuple-element.51.second, bf16[256,256]{1,0:T(8,128)(2,1)S(1)} %get-tuple-element.52.m_high, ...), custom_call_target="tpu_custom_call" | custom-call | tf_op jit(solution)/shard_map/chain/pallas_call | solution.py:377
  4.6 0.0 copy-start
  4.6 1.6 %collective-permute-start.2 = (bf16[8,128]{1,0:T(8,128)(2,1)S(1)}, bf16[8,128]{1,0:T(8,128)(2,1)S(1)}, u32[]{:S(2)}, u32[]{:S(2)}) collective-permute-start(bf16[8,128]{1,0:T(8,128)(2,1)S(1)} %get-tuple-element.57), channel_id=1, source_target_pairs={{0,4},{4,0},{8,12},{12,8},{1,5},{5,1},{9,13},{13,9},{2,6},{6,2},{1... | collective-permute-start | bytes 6152 | tf_op jit(solution)/shard_map/ppermute | solution.py:389
  6.3 2.6 %collective-permute-start.3 = (bf16[8,128]{1,0:T(8,128)(2,1)S(1)}, bf16[8,128]{1,0:T(8,128)(2,1)S(1)}, u32[]{:S(2)}, u32[]{:S(2)}) collective-permute-start(bf16[8,128]{1,0:T(8,128)(2,1)S(1)} %get-tuple-element.59), channel_id=1, source_target_pairs={{0,8},{4,12},{8,4},{12,0},{1,9},{5,13},{9,5},{13,1},{2,10},{6,14},... | collective-permute-start | bytes 6152 | tf_op jit(solution)/shard_map/ppermute | solution.py:389
  8.9 1.2 %collective-permute-start.4 = (bf16[8,128]{1,0:T(8,128)(2,1)S(1)}, bf16[8,128]{1,0:T(8,128)(2,1)S(1)}, u32[]{:S(2)}, u32[]{:S(2)}) collective-permute-start(bf16[8,128]{1,0:T(8,128)(2,1)S(1)} %get-tuple-element.60), channel_id=1, source_target_pairs={{0,12},{4,8},{8,0},{12,4},{1,13},{5,9},{9,1},{13,5},{2,14},{6,10},... | collective-permute-start | bytes 6152 | tf_op jit(solution)/shard_map/ppermute | solution.py:389
  10.1 0.0 copy-done.1
  10.1 0.0 copy-done
  10.1 0.8 %place.1.refs_3_.refs_2_ = bf16[512,256]{1,0:T(8,128)(2,1)S(1)} custom-call(s32[4,4]{1,0:T(4,128)S(1)} %copy-done, bf16[4,32,256]{2,1,0:T(8,128)(2,1)S(1)} %copy-done.1), custom_call_target="tpu_custom_call" | custom-call | flops 100000000 | bytes 400000 | tf_op jit(solution)/shard_map/place/pallas_call | solution.py:392
  10.9 0.8 %collective-permute-done.3.refs_1_ = bf16[8,128]{1,0:T(8,128)(2,1)S(1)} collective-permute-done((bf16[8,128]{1,0:T(8,128)(2,1)S(1)}, bf16[8,128]{1,0:T(8,128)(2,1)S(1)}, u32[]{:S(2)}, u32[]{:S(2)}) %collective-permute-start.3) | collective-permute-done | bytes 2080 | tf_op jit(solution)/shard_map/ppermute | solution.py:389
  11.6 1.7 %collective-permute-done.4.refs_2_ = bf16[8,128]{1,0:T(8,128)(2,1)S(1)} collective-permute-done((bf16[8,128]{1,0:T(8,128)(2,1)S(1)}, bf16[8,128]{1,0:T(8,128)(2,1)S(1)}, u32[]{:S(2)}, u32[]{:S(2)}) %collective-permute-start.4) | collective-permute-done | bytes 2080 | tf_op jit(solution)/shard_map/ppermute | solution.py:389
  13.3 0.1 partial.1.refs_1_
  13.5 0.0 collective-permute-done.2.refs_0_
  13.5 0.8 %finish.1 = f32[8,256]{1,0:T(8,128)} custom-call(bf16[8,128]{1,0:T(8,128)(2,1)S(1)} %collective-permute-done.2.refs_0_, f32[8,256]{1,0:T(8,128)S(1)} %partial.1.refs_1_, bf16[512,256]{1,0:T(8,128)(2,1)S(1)} %place.1.refs_3_.refs_2_), custom_call_target="tpu_custom_call" | custom-call | tf_op jit(solution)/shard_map/finish/pallas_call | solution.py:411
Async XLA Ops:
  0.9 3.4 %collective-permute-start.1 = (bf16[4,2560]{1,0:T(4,128)(2,1)S(1)}, bf16[4,2560]{1,0:T(4,128)(2,1)S(1)}, u32[]{:S(2)}, u32[]{:S(2)}) collective-permute-start(bf16[4,2560]{1,0:T(4,128)(2,1)S(1)} %get-tuple-element.47), channel_id=1, source_target_pairs={{0,1},{1,0},{2,3},{3,2},{4,5},{5,4},{6,7},{7,6},{8,9},{9,8},{10,11... | collective-permute-start | bytes 61448 | tf_op jit(solution)/shard_map/ppermute | solution.py:366
  1.0 3.3 %collective-permute-start = (bf16[4,2560]{1,0:T(4,128)(2,1)S(1)}, bf16[4,2560]{1,0:T(4,128)(2,1)S(1)}, u32[]{:S(2)}, u32[]{:S(2)}) collective-permute-start(bf16[4,2560]{1,0:T(4,128)(2,1)S(1)} %get-tuple-element.17), channel_id=1, source_target_pairs={{1,2},{2,1},{3,0},{0,3},{5,6},{6,5},{7,4},{4,7},{9,10},{10,9},{11,... | collective-permute-start | bytes 61448 | tf_op jit(solution)/shard_map/cond/branch_0_fun/ppermute | solution.py:372
  4.3 5.8 %copy-start.1 = (bf16[4,32,256]{2,1,0:T(8,128)(2,1)S(1)}, bf16[4,32,256]{2,1,0:T(8,128)(2,1)}, u32[]{:S(2)}) copy-start(bf16[4,32,256]{2,1,0:T(8,128)(2,1)} %weights.1) | copy-start | bytes 196612
  4.6 5.5 %copy-start = (s32[4,4]{1,0:T(4,128)S(1)}, s32[4,4]{1,0:T(4,128)}, u32[]{:S(2)}) copy-start(s32[4,4]{1,0:T(4,128)} %starts.1) | copy-start | bytes 196
  4.6 8.8 %collective-permute-start.2 = (bf16[8,128]{1,0:T(8,128)(2,1)S(1)}, bf16[8,128]{1,0:T(8,128)(2,1)S(1)}, u32[]{:S(2)}, u32[]{:S(2)}) collective-permute-start(bf16[8,128]{1,0:T(8,128)(2,1)S(1)} %get-tuple-element.57), channel_id=1, source_target_pairs={{0,4},{4,0},{8,12},{12,8},{1,5},{5,1},{9,13},{13,9},{2,6},{6,2},{1... | collective-permute-start | bytes 6152 | tf_op jit(solution)/shard_map/ppermute | solution.py:389
  6.3 5.4 %collective-permute-start.3 = (bf16[8,128]{1,0:T(8,128)(2,1)S(1)}, bf16[8,128]{1,0:T(8,128)(2,1)S(1)}, u32[]{:S(2)}, u32[]{:S(2)}) collective-permute-start(bf16[8,128]{1,0:T(8,128)(2,1)S(1)} %get-tuple-element.59), channel_id=1, source_target_pairs={{0,8},{4,12},{8,4},{12,0},{1,9},{5,13},{9,5},{13,1},{2,10},{6,14},... | collective-permute-start | bytes 6152 | tf_op jit(solution)/shard_map/ppermute | solution.py:389
  8.9 4.5 %collective-permute-start.4 = (bf16[8,128]{1,0:T(8,128)(2,1)S(1)}, bf16[8,128]{1,0:T(8,128)(2,1)S(1)}, u32[]{:S(2)}, u32[]{:S(2)}) collective-permute-start(bf16[8,128]{1,0:T(8,128)(2,1)S(1)} %get-tuple-element.60), channel_id=1, source_target_pairs={{0,12},{4,8},{8,0},{12,4},{1,13},{5,9},{9,1},{13,5},{2,14},{6,10},... | collective-permute-start | bytes 6152 | tf_op jit(solution)/shard_map/ppermute | solution.py:389
